TPU v7x, 512 devices: a whole 4x8x8 slice. The times are simulated.
512 devices in a mesh: lon: 64 (over z_lo, y, core), lat: 8 (over x, z_hi).
Axes of the slice: x: 4, y: 8, z: 8 (z_hi: 2, z_lo: 4; z = z_hi * 4 + z_lo), core: 2. Of those that a mesh axis runs over, the one named last changes fastest.
Arguments:
- prediction: bfloat16 [384, 1536, 222], P('lat', 'lon'), may hold values from -40 to 40
- observed_state: bfloat16 [384, 1536, 222], P('lat', 'lon'), may hold values from -40 to 40
- mean_state: bfloat16 [384, 1536, 222], P('lat', 'lon'), may hold values from -6 to 6
- usable_point_flags: int32 [384, 1536], P('lat', 'lon'), may hold values 0 or 1
- eastward_offsets: int32 [8], replicated, may hold values from 0 to 335, as said below
Outputs:
- correlation: float32 [8, 1536, 222], P('lat', 'lon')
Inputs may be any that keep to these rules, and one draw needn't show every extreme that they name: `eastward_offsets`: every lag lies below 336, and some lag equals 335.
All inputs are finite; a program needn't handle non-finite values. No bound on the sum of `usable_point_flags` on one device may be relied on, other than what follows from the above.
Results may differ from a plain program's by a relative error of at most 0.0044.
Values may be sent and summed in bfloat16 or wider, within the bound.
No kernel may reach another device: no remote copies, remote signals or barrier semaphores. Data moves between devices by JAX's collectives and lax.ppermute only.
A program may use at most 64 MiB of HBM per device.

v0:
```python
import jax
import jax.numpy as jnp
import numpy as np
from jax import lax
from jax.experimental import pallas as pl
from jax.experimental.pallas import tpu as pltpu
from jax.sharding import Mesh
from jax.sharding import PartitionSpec as P

REG = 0.001
K = 8
ROWS = 48
COLS = 24
TILES = COLS // 8
CHANNELS = 222
GROUPS = 16
PER = 14
SIDE = 9
STEPS = 5
TAIL = ROWS - STEPS * SIDE
PACKED = STEPS * COLS + 8
BLOCK = GROUPS * COLS
HALO = 14
WINDOW = BLOCK + HALO * COLS
MISSING = 1024.0
LANES = 128


def pack_kernel(field_ref, mean_ref, flags_ref, out_ref, field, mean, flags, low, mid, high, packed, arrived, leaving):
    def rows_of(g):
        return pl.ds(g * SIDE, SIDE if g < STEPS else TAIL)

    def fetch(g):
        rows = rows_of(g)
        return (
            pltpu.make_async_copy(field_ref.at[rows], field.at[rows], arrived.at[0, g]),
            pltpu.make_async_copy(mean_ref.at[rows], mean.at[rows], arrived.at[1, g]),
        )

    def leave(g):
        rows = pl.ds(g * COLS, COLS if g < STEPS else 8)
        return pltpu.make_async_copy(packed.at[:, rows, :], out_ref.at[:, rows, :], leaving.at[g])

    fetch_flags = pltpu.make_async_copy(flags_ref, flags, arrived.at[2, 0])
    fetch_flags.start()
    for g in range(STEPS + 1):
        for copy in fetch(g):
            copy.start()
    lane = lax.broadcasted_iota(jnp.int32, (8, LANES), 1)
    pad = jnp.zeros((COLS, 2 * LANES - CHANNELS), jnp.float32)
    fetch_flags.wait()
    valid = flags[...].astype(jnp.float32)

    def anomaly(row, keep):
        left = field[row, :, :LANES].astype(jnp.float32) - mean[row, :, :LANES].astype(jnp.float32)
        right = field[row, :, LANES:].astype(jnp.float32) - mean[row, :, LANES:].astype(jnp.float32)
        keep = jnp.broadcast_to(keep, (COLS, LANES)) > 0.5
        return jnp.where(keep, left, MISSING), jnp.where(keep, jnp.concatenate([right, pad], axis=1), MISSING)

    def place(turn, at, part, left, right):
        left, right = pltpu.roll(left, PER * at, 1), pltpu.roll(right, PER * at, 1)
        low[turn, at, part], high[turn, at, part] = left, right
        mid[turn, at, part] = jnp.where(((lane - PER * at) & (LANES - 1)) >= 9 * PER, left, right)

    def take(g):
        for copy in fetch(g):
            copy.wait()
        count = SIDE if g < STEPS else TAIL
        for row in range(count):
            at = g * SIDE + row
            left, right = anomaly(at, valid[:, at : at + 1])
            for part in range(TILES):
                slot, tile = (row, part) if g < STEPS else (part * TAIL + row, 0)
                rows = slice(part * 8, part * 8 + 8)
                place(g % 2, slot, tile, left[rows], right[rows])

    def emit(g):
        for q in range(GROUPS):
            source = low if q < 9 else mid if q == 9 else high
            slot = (lane - PER * q) & (LANES - 1)
            for part in range(TILES if g < STEPS else 1):
                acc = source[g % 2, 0, part]
                for at in range(1, SIDE):
                    acc = jnp.where(slot >= PER * at, source[g % 2, at, part], acc)
                moved = pltpu.roll(acc, -PER * q % LANES, 1)
                packed[q, pl.ds(g * COLS + part * 8, 8), :] = moved.astype(jnp.bfloat16)
        leave(g).start()

    take(0)
    for g in range(STEPS + 1):
        if g < STEPS:
            take(g + 1)
        emit(g)
    for g in range(STEPS + 1):
        leave(g).wait()


def on_chip(mib, flops):
    return dict(
        compiler_params=pltpu.CompilerParams(vmem_limit_bytes=mib * 1024 * 1024),
        cost_estimate=pl.CostEstimate(flops=flops, bytes_accessed=2_000_000, transcendentals=0),
    )


def pack(field, mean, flags):
    anywhere = pl.BlockSpec(memory_space=pl.ANY)
    return pl.pallas_call(
        pack_kernel,
        in_specs=[anywhere] * 3,
        out_specs=anywhere,
        out_shape=jax.ShapeDtypeStruct((GROUPS, PACKED, LANES), jnp.bfloat16),
        scratch_shapes=[pltpu.VMEM((ROWS, COLS, CHANNELS), jnp.bfloat16)] * 2
        + [pltpu.VMEM((COLS, ROWS), jnp.int32)]
        + [pltpu.VMEM((2, SIDE, TILES, 8, LANES), jnp.float32)] * 3
        + [pltpu.VMEM((GROUPS, PACKED, LANES), jnp.bfloat16)]
        + [pltpu.SemaphoreType.DMA((3, STEPS + 1)), pltpu.SemaphoreType.DMA((STEPS + 1,))],
        name="pack",
        **on_chip(62, 4_000_000),
    )(field, mean, flags)


def totals_at(k, t):
    return pl.ds(pl.multiple_of((t * K + k) * 8, 8), 8)


def halves_of(value):
    first = value.astype(jnp.bfloat16)
    return first, (value - first.astype(jnp.float32)).astype(jnp.bfloat16)


OWN = (STEPS + 1) * BLOCK
OWN_STRIDE = OWN + 8
WINDOW_STRIDE = (STEPS + 1) * WINDOW + 16


def gather_matrix(n):
    row = lax.broadcasted_iota(jnp.int32, (3 * LANES, LANES), 0)
    lane = lax.broadcasted_iota(jnp.int32, (3 * LANES, LANES), 1)
    source = row & (LANES - 1)
    channel = source
    for at in range(1, SIDE + 1):
        channel = jnp.where(source >= PER * at, source - PER * at, channel)
    target = channel + PER * (TILES * n + row // LANES)
    return jnp.where((source < PER * SIDE) & (lane == target), 1.0, 0.0).astype(jnp.bfloat16)


def dot(a, b):
    return jnp.dot(a, b, preferred_element_type=jnp.float32)


def sums_kernel(offsets_ref, weight_ref, fore_ref, true_ref, next_ref, out_ref, held, window, total):
    cross, spread, weigh = (held.at[pl.ds(n * OWN_STRIDE, OWN)] for n in range(3))
    shifted, usable = (window.at[pl.ds(n * WINDOW_STRIDE, (STEPS + 1) * WINDOW)] for n in range(2))
    lane = lax.broadcasted_iota(jnp.int32, (8, LANES), 1)

    def unpack(source, first):
        def tile(g, part, p, value, fore):
            at = pl.ds(pl.multiple_of(g * WINDOW + first + p * COLS + part * 8, 8), 8)
            keep = value < MISSING / 2
            shifted[at, :] = jnp.where(keep, value, 0.0)
            usable[at, :] = jnp.where(keep, 1.0, 0.0)
            if first == 0:
                at = pl.ds(pl.multiple_of(g * BLOCK + p * COLS + part * 8, 8), 8)
                masked = jnp.where(keep, weight_ref[g : g + 1, :], 0.0)
                scaled = fore * masked
                weigh[at, :] = masked
                cross[at, :] = scaled
                spread[at, :] = scaled * fore

        def run(p, carry):
            for g in range(STEPS):
                rows = slice(g * COLS, (g + 1) * COLS)
                value = source[p, rows, :].astype(jnp.float32)
                fore = fore_ref[p, rows, :].astype(jnp.float32) if first == 0 else value
                for part in range(TILES):
                    tile(g, part, p, value[part * 8 : part * 8 + 8], fore[part * 8 : part * 8 + 8])
            rows = slice(STEPS * COLS, PACKED)
            value = source[p, rows, :].astype(jnp.float32)
            fore = fore_ref[p, rows, :].astype(jnp.float32) if first == 0 else value
            for part in range(TILES):
                turn = -PER * TAIL * part % LANES
                moved = pltpu.roll(value, turn, 1) if part else value
                moved = jnp.where(lane < PER * TAIL, moved, MISSING)
                tile(STEPS, part, p, moved, pltpu.roll(fore, turn, 1) if part else fore)
            return carry

        return run

    lax.fori_loop(0, GROUPS, unpack(true_ref, 0), 0, unroll=8)
    lax.fori_loop(0, HALO, unpack(next_ref, BLOCK), 0, unroll=14)
    lag = [offsets_ref[k] for k in range(K)]

    def tile(t, carry):
        for part in range(TILES):
            start = t * COLS + part * 8
            acc = [[jnp.zeros((8, LANES), jnp.float32)] * 3 for _ in range(K)]
            for g in range(STEPS + 1):
                at = pl.ds(pl.multiple_of(g * BLOCK + start, 8), 8)
                a, c, d = cross[at, :], spread[at, :], weigh[at, :]
                for k in range(K):
                    there = pl.ds(g * WINDOW + start + lag[k], 8)
                    b, v = shifted[there, :], usable[there, :]
                    acc[k] = [acc[k][0] + a * b, acc[k][1] + c * v, acc[k][2] + d * (b * b)]
            for k in range(K):
                for n in range(3):
                    column = (n * TILES + part) * LANES
                    total[totals_at(k, t), column : column + LANES] = acc[k][n]
        return carry

    lax.fori_loop(0, GROUPS, tile, 0)
    first, second = halves_of(total[:, : 3 * LANES])
    gather = gather_matrix(0)
    out = dot(first, gather) + dot(second, gather)
    for n in range(1, 3):
        out += dot(total[:, 3 * n * LANES : 3 * (n + 1) * LANES].astype(jnp.bfloat16), gather_matrix(n))
    out_ref[...] = out.astype(jnp.bfloat16)


SCRATCH = ((3 * OWN_STRIDE, LANES), (2 * WINDOW_STRIDE, LANES), (K * GROUPS * 8, 9 * LANES))


def window_call(kernel, inputs, scratch, name, flops):
    vmem = pl.BlockSpec(memory_space=pltpu.VMEM)
    return pl.pallas_call(
        kernel,
        in_specs=[pl.BlockSpec(memory_space=pltpu.SMEM)] + [vmem] * (len(inputs) - 1),
        out_specs=vmem,
        out_shape=jax.ShapeDtypeStruct((K * GROUPS * 8, LANES), jnp.bfloat16),
        scratch_shapes=[pltpu.VMEM((rows, lanes), jnp.float32) for rows, lanes in scratch],
        name=name,
        **on_chip(28, flops),
    )(*inputs)


def finish_kernel(parts_ref, out_ref):
    lane = lax.broadcasted_iota(jnp.int32, (8, LANES), 1)
    halves = [[jnp.zeros((8, LANES), jnp.float32)] * 2 for _ in range(3)]
    for q in range(GROUPS):
        total = parts_ref[q * K].astype(jnp.float32)
        for device in range(1, K):
            total = total + parts_ref[q * K + device].astype(jnp.float32)
        fore = pltpu.roll(total, LANES - 3 * PER, 1)
        true = pltpu.roll(total, LANES - 6 * PER, 1)
        value = total / jnp.sqrt((fore + REG) * (true + REG))
        low, high = PER * q, PER * q + PER
        for part in range(3):
            moved = pltpu.roll(value, (PER * q - PER * part) % LANES, 1)
            for half in range(2):
                at = lane + half * LANES
                if low < (half + 1) * LANES and high > half * LANES:
                    halves[part][half] = jnp.where((at >= low) & (at < high), moved, halves[part][half])
    for part in range(3):
        out_ref[0, part * 8 : part * 8 + 8, :LANES] = halves[part][0]
        out_ref[0, part * 8 : part * 8 + 8, LANES:] = halves[part][1][:, : CHANNELS - LANES]


def finish(parts):
    vmem = pl.BlockSpec(memory_space=pltpu.VMEM)
    return pl.pallas_call(
        finish_kernel,
        in_specs=[vmem],
        out_specs=vmem,
        out_shape=jax.ShapeDtypeStruct((1, COLS, CHANNELS), jnp.float32),
        name="finish",
        **on_chip(4, 1_000_000),
    )(parts)


def local(prediction, observed_state, mean_state, usable_point_flags, eastward_offsets):
    place = np.arange(STEPS + 1)[:, None] * SIDE + np.arange(LANES)[None, :] // PER
    inside = (np.arange(LANES)[None, :] < PER * SIDE) & (place < ROWS)
    row = (lax.axis_index("lat") * ROWS + place).astype(jnp.float32)
    weight = jnp.cos(jnp.pi * ((row + 0.5) / (ROWS * lax.axis_size("lat")) - 0.5))
    weight = jnp.where(inside, weight, 0.0)
    flags = usable_point_flags.T
    around = ("y", "core")
    true = pack(observed_state, mean_state, flags)
    true = lax.all_to_all(true, around, 0, 0, tiled=True)
    count = lax.axis_size("z")
    following = lax.ppermute(true[:HALO], "z", [((i + 1) % count, i) for i in range(count)])
    fore = pack(prediction, mean_state, flags)
    fore = lax.all_to_all(fore, around, 0, 0, tiled=True)
    sums = window_call(
        sums_kernel,
        (eastward_offsets, weight, fore, true, following),
        SCRATCH,
        "lag_sums",
        20_000_000,
    )
    parts = sums.reshape(K * GROUPS, 8, LANES)
    parts = lax.all_to_all(parts, around + ("lat",), 0, 0, tiled=True)
    return finish(parts)


def solution(mesh):
    split = Mesh(mesh.devices.reshape(4, 8, 2, 8), ("z", "y", "core", "lat"))
    lon = ("z", "y", "core")
    placed = (P("lat", lon, None), P("lat", lon, None), P("lat", lon, None), P("lat", lon), P())
    return jax.shard_map(local, mesh=split, in_specs=placed, out_specs=P("lat", lon, None), check_vma=False)
```

profile of v0, /device:TPU:1, one launch (start us, length us, event | category | flops | bytes accessed | tf_op | source)
XLA Modules:
  0.0 91.2 jit_solution(2026257797954579751)
XLA Ops:
  0.0 3.5 %pack.3 = bf16[16,128,128]{2,1,0:T(8,128)(2,1)} custom-call(bf16[48,24,222]{2,1,0:T(8,128)(2,1)} %field_ref.3, bf16[48,24,222]{2,1,0:T(8,128)(2,1)} %mean_ref.3, s32[24,48]{1,0:T(8,128)} %bitcast.3), custom_call_target="tpu_custom_call" | custom-call | flops 4000000 | bytes 2000000 | tf_op jit(solution)/shard_map/pack/pallas_call | solution.py:107
  3.5 10.2 %all-to-all-start.1 = ((bf16[16,128,128]{2,1,0:T(8,128)(2,1)}), bf16[16,128,128]{2,1,0:T(8,128)(2,1)S(1)}, u32[]{:S(2)}, u32[]{:S(2)}) async-start(bf16[16,128,128]{2,1,0:T(8,128)(2,1)} %pack.3), calls=%async_computation.1 | async-start | bytes 1048576 | tf_op jit(solution)/shard_map/all_to_all | solution.py:278
  13.7 3.6 %pack.2 = bf16[16,128,128]{2,1,0:T(8,128)(2,1)} custom-call(bf16[48,24,222]{2,1,0:T(8,128)(2,1)} %field_ref.2, bf16[48,24,222]{2,1,0:T(8,128)(2,1)} %mean_ref.3, s32[24,48]{1,0:T(8,128)} %bitcast.4), custom_call_target="tpu_custom_call" | custom-call | flops 4000000 | bytes 2000000 | tf_op jit(solution)/shard_map/pack/pallas_call | solution.py:107
  17.3 13.7 %all-to-all-done.1.true_ref = bf16[16,128,128]{2,1,0:T(8,128)(2,1)S(1)} async-done(((bf16[16,128,128]{2,1,0:T(8,128)(2,1)}), bf16[16,128,128]{2,1,0:T(8,128)(2,1)S(1)}, u32[]{:S(2)}, u32[]{:S(2)}) %all-to-all-start.1) | async-done | bytes 524320 | tf_op jit(solution)/shard_map/all_to_all | solution.py:278
  31.1 3.5 %all-to-all-start = ((bf16[16,128,128]{2,1,0:T(8,128)(2,1)}), bf16[16,128,128]{2,1,0:T(8,128)(2,1)S(1)}, u32[]{:S(2)}, u32[]{:S(2)}) async-start(bf16[16,128,128]{2,1,0:T(8,128)(2,1)} %pack.2), calls=%async_computation | async-start | bytes 1048576 | tf_op jit(solution)/shard_map/all_to_all | solution.py:282
  34.6 0.0 copy-start.1
  34.6 5.9 %collective-permute-start = (bf16[14,128,128]{2,1,0:T(8,128)(2,1)S(1)}, bf16[14,128,128]{2,1,0:T(8,128)(2,1)S(1)}, u32[]{:S(2)}, u32[]{:S(2)}) collective-permute-start(bf16[14,128,128]{2,1,0:T(8,128)(2,1)S(1)} %slice.4), channel_id=1, source_target_pairs={{128,0},{256,128},{384,256},{0,384},{129,1},{257,129},{385,257},{1... | collective-permute-start | bytes 1376264 | tf_op jit(solution)/shard_map/ppermute | solution.py:280
  40.5 0.0 copy-start.2
  40.5 0.0 copy-done.1
  40.5 0.7 copy-done.2
  41.2 0.0 copy-start
  41.2 9.9 %all-to-all-done.fore_ref = bf16[16,128,128]{2,1,0:T(8,128)(2,1)S(1)} async-done(((bf16[16,128,128]{2,1,0:T(8,128)(2,1)}), bf16[16,128,128]{2,1,0:T(8,128)(2,1)S(1)}, u32[]{:S(2)}, u32[]{:S(2)}) %all-to-all-start) | async-done | bytes 524320 | tf_op jit(solution)/shard_map/all_to_all | solution.py:282
  51.2 0.0 collective-permute-done.next_ref
  51.2 0.0 copy-done
  51.2 4.8 %lag_sums.1 = bf16[1024,128]{1,0:T(8,128)(2,1)S(1)} custom-call(s32[8]{0:T(128)S(1)} %copy-done, f32[6,128]{1,0:T(8,128)S(1)} %cosine_select_fusion.weight_ref, bf16[16,128,128]{2,1,0:T(8,128)(2,1)S(1)} %all-to-all-done.fore_ref, bf16[16,128,128]{2,1,0:T(8,128)(2,1)S(1)} %all-to-all-done.1.true_ref, bf16[14,128,128]{2,1,0:T(8,128)(2,1)S(1)} %collective-permute-done.next_ref), custom_call_target="tpu_custom_call" | custom-call | flops 20000000 | bytes 2000000 | tf_op jit(solution)/shard_map/lag_sums/pallas_call | solution.py:224
  56.0 34.4 %all_to_all.15.parts_ref = bf16[128,8,128]{2,1,0:T(8,128)(2,1)S(1)} all-to-all(bf16[128,8,128]{2,1,0:T(8,128)(2,1)S(1)} %bitcast.2), channel_id=1, replica_groups=mesh['z'=4,'y'=8,'core'=2,'lat'=8] {'y','core','lat'}, dimensions={0} | all-to-all | bytes 524288 | tf_op jit(solution)/shard_map/all_to_all | solution.py:291
  90.4 0.8 finish.1
  (2 shorter events, 0.1 us)
Async XLA Ops:
  3.5 27.5 %all-to-all-start.1 = ((bf16[16,128,128]{2,1,0:T(8,128)(2,1)}), bf16[16,128,128]{2,1,0:T(8,128)(2,1)S(1)}, u32[]{:S(2)}, u32[]{:S(2)}) async-start(bf16[16,128,128]{2,1,0:T(8,128)(2,1)} %pack.3), calls=%async_computation.1 | async-start | bytes 1048576 | tf_op jit(solution)/shard_map/all_to_all | solution.py:278
  31.1 20.1 %all-to-all-start = ((bf16[16,128,128]{2,1,0:T(8,128)(2,1)}), bf16[16,128,128]{2,1,0:T(8,128)(2,1)S(1)}, u32[]{:S(2)}, u32[]{:S(2)}) async-start(bf16[16,128,128]{2,1,0:T(8,128)(2,1)} %pack.2), calls=%async_computation | async-start | bytes 1048576 | tf_op jit(solution)/shard_map/all_to_all | solution.py:282
  34.6 6.0 %copy-start.1 = (s32[6,128]{1,0:T(8,128)S(1)}, s32[6,128]{1,0:T(8,128)}, u32[]{:S(2)}) copy-start(s32[6,128]{1,0:T(8,128)} %constant.21.clone) | copy-start | bytes 9220
  34.6 16.6 %collective-permute-start = (bf16[14,128,128]{2,1,0:T(8,128)(2,1)S(1)}, bf16[14,128,128]{2,1,0:T(8,128)(2,1)S(1)}, u32[]{:S(2)}, u32[]{:S(2)}) collective-permute-start(bf16[14,128,128]{2,1,0:T(8,128)(2,1)S(1)} %slice.4), channel_id=1, source_target_pairs={{128,0},{256,128},{384,256},{0,384},{129,1},{257,129},{385,257},{1... | collective-permute-start | bytes 1376264 | tf_op jit(solution)/shard_map/ppermute | solution.py:280
  40.5 0.7 copy-start.2
  41.2 10.0 %copy-start = (s32[8]{0:T(128)S(1)}, s32[8]{0:T(128)}, u32[]{:S(2)}) copy-start(s32[8]{0:T(128)} %offsets_ref.1) | copy-start | bytes 100
where the time goes:
time: 91.7 us; the launch traced here: 91.2 us
  blocking collectives  34.4 us (38%)
  waiting for transfers between devices  23.7 us (26%)
  starting transfers between devices  19.6 us (21%)
  Pallas kernels  12.7 us (14%)
    all_to_all x1, blocking collectives, local(): parts = lax.all_to_all(parts, around + ('lat',), 0, 0, tiled=True)  34.4 us
    all_to_all x1, waiting for transfers between devices, local(): true = lax.all_to_all(true, around, 0, 0, tiled=True)  13.7 us
    all_to_all x1, starting transfers between devices, local(): true = lax.all_to_all(true, around, 0, 0, tiled=True)  10.2 us
    all_to_all x1, waiting for transfers between devices, local(): fore = lax.all_to_all(fore, around, 0, 0, tiled=True)  9.92 us
    pallas_call x2, Pallas kernels, pack(): pl.pallas_call(pack_kernel, in_specs=[anywhere] * 3, out_specs=anywhere,...  7.08 us
    ppermute x1, starting transfers between devices, local(): lax.ppermute(true[:HALO], 'z', [((i + 1) % count, i) for i in range(count)])  5.92 us
    pallas_call x1, Pallas kernels, window_call(): pl.pallas_call(kernel, in_specs=[pl.BlockSpec(memory_space=pltpu.SMEM)] +...  4.79 us
    all_to_all x1, starting transfers between devices, local(): fore = lax.all_to_all(fore, around, 0, 0, tiled=True)  3.47 us
  transfers between devices with their start and end apart: 3, of which 2 were waited for; matrix products, arithmetic and copies ran while one was open for 0% of the time, Pallas kernels for 4%

commit v1 on v0

--- a/solution.py
+++ b/solution.py
@@ -120,7 +120,7 @@
 
 
 def totals_at(k, t):
-    return pl.ds(pl.multiple_of((t * K + k) * 8, 8), 8)
+    return pl.ds(pl.multiple_of(((t % 2 * 8 + t // 2) * K + k) * 8, 8), 8)
 
 
 def halves_of(value):
@@ -167,16 +167,19 @@
                 cross[at, :] = scaled
                 spread[at, :] = scaled * fore
 
-        def run(p, carry):
+        def run(turn, carry):
+            half = HALO // 2 if first else GROUPS // 2
+            core, line = turn // half, turn % half
+            source_block, p = core * 8 + line, line * 2 + core
             for g in range(STEPS):
                 rows = slice(g * COLS, (g + 1) * COLS)
-                value = source[p, rows, :].astype(jnp.float32)
-                fore = fore_ref[p, rows, :].astype(jnp.float32) if first == 0 else value
+                value = source[source_block, rows, :].astype(jnp.float32)
+                fore = fore_ref[source_block, rows, :].astype(jnp.float32) if first == 0 else value
                 for part in range(TILES):
                     tile(g, part, p, value[part * 8 : part * 8 + 8], fore[part * 8 : part * 8 + 8])
             rows = slice(STEPS * COLS, PACKED)
-            value = source[p, rows, :].astype(jnp.float32)
-            fore = fore_ref[p, rows, :].astype(jnp.float32) if first == 0 else value
+            value = source[source_block, rows, :].astype(jnp.float32)
+            fore = fore_ref[source_block, rows, :].astype(jnp.float32) if first == 0 else value
             for part in range(TILES):
                 turn = -PER * TAIL * part % LANES
                 moved = pltpu.roll(value, turn, 1) if part else value
@@ -273,11 +276,11 @@
     weight = jnp.cos(jnp.pi * ((row + 0.5) / (ROWS * lax.axis_size("lat")) - 0.5))
     weight = jnp.where(inside, weight, 0.0)
     flags = usable_point_flags.T
-    around = ("y", "core")
+    around = ("core", "y")
     true = pack(observed_state, mean_state, flags)
     true = lax.all_to_all(true, around, 0, 0, tiled=True)
     count = lax.axis_size("z")
-    following = lax.ppermute(true[:HALO], "z", [((i + 1) % count, i) for i in range(count)])
+    following = lax.ppermute(true, "z", [((i + 1) % count, i) for i in range(count)])
     fore = pack(prediction, mean_state, flags)
     fore = lax.all_to_all(fore, around, 0, 0, tiled=True)
     sums = window_call(

time: 91.7 us -> 92.9 us (1.013)
  starting transfers between devices: 19.6 us -> 21.7 us
  waiting for transfers between devices: 23.7 us -> 21.6 us
    all_to_all x1, waiting for transfers between devices: 13.7 us -> 11.2 us  [local(): true = lax.all_to_all(true, around, 0, 0, tiled=True)]
    ppermute x1, waiting for transfers between devices: 0.01 us -> 2.35 us  [local(): lax.ppermute(true, 'z', [((i + 1) % count, i) for i in range(count)])]
    all_to_all x1, starting transfers between devices: 3.47 us -> 5.45 us  [local(): fore = lax.all_to_all(fore, around, 0, 0, tiled=True)]
    all_to_all x1, waiting for transfers between devices: 9.92 us -> 8.07 us  [local(): fore = lax.all_to_all(fore, around, 0, 0, tiled=True)]
  transfers between devices with their start and end apart: 3 -> 3, of which waited for: 2 -> 3; matrix products, arithmetic and copies ran while one was open for 0% -> 0% of each run, Pallas kernels for 4% -> 4%
where the time goes in v1:
time: 92.9 us; the launch traced here: 92.5 us
  blocking collectives  35.2 us (38%)
  starting transfers between devices  21.7 us (23%)
  waiting for transfers between devices  21.6 us (23%)
  Pallas kernels  13.2 us (14%)
    all_to_all x1, blocking collectives, local(): parts = lax.all_to_all(parts, around + ('lat',), 0, 0, tiled=True)  35.2 us
    all_to_all x1, waiting for transfers between devices, local(): true = lax.all_to_all(true, around, 0, 0, tiled=True)  11.2 us
    all_to_all x1, starting transfers between devices, local(): true = lax.all_to_all(true, around, 0, 0, tiled=True)  10.3 us
    all_to_all x1, waiting for transfers between devices, local(): fore = lax.all_to_all(fore, around, 0, 0, tiled=True)  8.07 us
    pallas_call x2, Pallas kernels, pack(): pl.pallas_call(pack_kernel, in_specs=[anywhere] * 3, out_specs=anywhere,...  7.08 us
    ppermute x1, starting transfers between devices, local(): lax.ppermute(true, 'z', [((i + 1) % count, i) for i in range(count)])  5.95 us
    all_to_all x1, starting transfers between devices, local(): fore = lax.all_to_all(fore, around, 0, 0, tiled=True)  5.45 us
    pallas_call x1, Pallas kernels, window_call(): pl.pallas_call(kernel, in_specs=[pl.BlockSpec(memory_space=pltpu.SMEM)] +...  5.35 us
  transfers between devices with their start and end apart: 3, of which 3 were waited for; matrix products, arithmetic and copies ran while one was open for 0% of the time, Pallas kernels for 4%

profile of v1, /device:TPU:1, one launch (start us, length us, event | category | flops | bytes accessed | tf_op | source)
XLA Modules:
  0.0 92.5 jit_solution(16982429745731031415)
XLA Ops:
  0.0 3.5 %pack.3 = bf16[16,128,128]{2,1,0:T(8,128)(2,1)} custom-call(bf16[48,24,222]{2,1,0:T(8,128)(2,1)} %field_ref.3, bf16[48,24,222]{2,1,0:T(8,128)(2,1)} %mean_ref.3, s32[24,48]{1,0:T(8,128)} %bitcast.3), custom_call_target="tpu_custom_call" | custom-call | flops 4000000 | bytes 2000000 | tf_op jit(solution)/shard_map/pack/pallas_call | solution.py:107
  3.5 10.3 %all-to-all-start.1 = ((bf16[16,128,128]{2,1,0:T(8,128)(2,1)}), bf16[16,128,128]{2,1,0:T(8,128)(2,1)S(1)}, u32[]{:S(2)}, u32[]{:S(2)}) async-start(bf16[16,128,128]{2,1,0:T(8,128)(2,1)} %pack.3), calls=%async_computation.1 | async-start | bytes 1048576 | tf_op jit(solution)/shard_map/all_to_all | solution.py:281
  13.8 3.6 %pack.2 = bf16[16,128,128]{2,1,0:T(8,128)(2,1)} custom-call(bf16[48,24,222]{2,1,0:T(8,128)(2,1)} %field_ref.2, bf16[48,24,222]{2,1,0:T(8,128)(2,1)} %mean_ref.3, s32[24,48]{1,0:T(8,128)} %bitcast.4), custom_call_target="tpu_custom_call" | custom-call | flops 4000000 | bytes 2000000 | tf_op jit(solution)/shard_map/pack/pallas_call | solution.py:107
  17.4 11.2 %all-to-all-done.1.true_ref = bf16[16,128,128]{2,1,0:T(8,128)(2,1)S(1)} async-done(((bf16[16,128,128]{2,1,0:T(8,128)(2,1)}), bf16[16,128,128]{2,1,0:T(8,128)(2,1)S(1)}, u32[]{:S(2)}, u32[]{:S(2)}) %all-to-all-start.1) | async-done | bytes 524320 | tf_op jit(solution)/shard_map/all_to_all | solution.py:281
  28.6 5.4 %all-to-all-start = ((bf16[16,128,128]{2,1,0:T(8,128)(2,1)}), bf16[16,128,128]{2,1,0:T(8,128)(2,1)S(1)}, u32[]{:S(2)}, u32[]{:S(2)}) async-start(bf16[16,128,128]{2,1,0:T(8,128)(2,1)} %pack.2), calls=%async_computation | async-start | bytes 1048576 | tf_op jit(solution)/shard_map/all_to_all | solution.py:285
  34.0 0.0 copy-start.1
  34.0 6.0 %collective-permute-start = (bf16[16,128,128]{2,1,0:T(8,128)(2,1)S(1)}, bf16[16,128,128]{2,1,0:T(8,128)(2,1)S(1)}, u32[]{:S(2)}, u32[]{:S(2)}) collective-permute-start(bf16[16,128,128]{2,1,0:T(8,128)(2,1)S(1)} %all-to-all-done.1.true_ref), channel_id=1, source_target_pairs={{128,0},{256,128},{384,256},{0,384},{129,1},{257,129},{385,257},{1... | collective-permute-start | bytes 1572872 | tf_op jit(solution)/shard_map/ppermute | solution.py:283
  40.0 0.0 copy-start.2
  40.0 0.0 copy-done.1
  40.0 0.7 copy-done.2
  40.7 0.0 copy-start
  40.7 8.1 %all-to-all-done.fore_ref = bf16[16,128,128]{2,1,0:T(8,128)(2,1)S(1)} async-done(((bf16[16,128,128]{2,1,0:T(8,128)(2,1)}), bf16[16,128,128]{2,1,0:T(8,128)(2,1)S(1)}, u32[]{:S(2)}, u32[]{:S(2)}) %all-to-all-start) | async-done | bytes 524320 | tf_op jit(solution)/shard_map/all_to_all | solution.py:285
  48.8 2.4 %collective-permute-done.next_ref = bf16[16,128,128]{2,1,0:T(8,128)(2,1)S(1)} collective-permute-done((bf16[16,128,128]{2,1,0:T(8,128)(2,1)S(1)}, bf16[16,128,128]{2,1,0:T(8,128)(2,1)S(1)}, u32[]{:S(2)}, u32[]{:S(2)}) %collective-permute-start) | collective-permute-done | bytes 524320 | tf_op jit(solution)/shard_map/ppermute | solution.py:283
  51.1 0.0 copy-done
  51.1 5.3 %lag_sums.1 = bf16[1024,128]{1,0:T(8,128)(2,1)S(1)} custom-call(s32[8]{0:T(128)S(1)} %copy-done, f32[6,128]{1,0:T(8,128)S(1)} %cosine_select_fusion.weight_ref, bf16[16,128,128]{2,1,0:T(8,128)(2,1)S(1)} %all-to-all-done.fore_ref, bf16[16,128,128]{2,1,0:T(8,128)(2,1)S(1)} %all-to-all-done.1.true_ref, bf16[16,128,128]{2,1,0:T(8,128)(2,1)S(1)} %collective-permute-done.next_ref), custom_call_target="tpu_custom_call" | custom-call | flops 20000000 | bytes 2000000 | tf_op jit(solution)/shard_map/lag_sums/pallas_call | solution.py:227
  56.5 35.2 %all_to_all.15.parts_ref = bf16[128,8,128]{2,1,0:T(8,128)(2,1)S(1)} all-to-all(bf16[128,8,128]{2,1,0:T(8,128)(2,1)S(1)} %bitcast.2), channel_id=1, replica_groups=mesh['z'=4,'y'=8,'core'=2,'lat'=8] {'core','y','lat'}, dimensions={0} | all-to-all | bytes 524288 | tf_op jit(solution)/shard_map/all_to_all | solution.py:294
  91.7 0.8 finish.1
  (1 shorter events, 0.0 us)
Async XLA Ops:
  3.5 25.0 %all-to-all-start.1 = ((bf16[16,128,128]{2,1,0:T(8,128)(2,1)}), bf16[16,128,128]{2,1,0:T(8,128)(2,1)S(1)}, u32[]{:S(2)}, u32[]{:S(2)}) async-start(bf16[16,128,128]{2,1,0:T(8,128)(2,1)} %pack.3), calls=%async_computation.1 | async-start | bytes 1048576 | tf_op jit(solution)/shard_map/all_to_all | solution.py:281
  28.6 20.2 %all-to-all-start = ((bf16[16,128,128]{2,1,0:T(8,128)(2,1)}), bf16[16,128,128]{2,1,0:T(8,128)(2,1)S(1)}, u32[]{:S(2)}, u32[]{:S(2)}) async-start(bf16[16,128,128]{2,1,0:T(8,128)(2,1)} %pack.2), calls=%async_computation | async-start | bytes 1048576 | tf_op jit(solution)/shard_map/all_to_all | solution.py:285
  34.0 6.0 %copy-start.1 = (s32[6,128]{1,0:T(8,128)S(1)}, s32[6,128]{1,0:T(8,128)}, u32[]{:S(2)}) copy-start(s32[6,128]{1,0:T(8,128)} %constant.21.clone) | copy-start | bytes 9220
  34.0 17.1 %collective-permute-start = (bf16[16,128,128]{2,1,0:T(8,128)(2,1)S(1)}, bf16[16,128,128]{2,1,0:T(8,128)(2,1)S(1)}, u32[]{:S(2)}, u32[]{:S(2)}) collective-permute-start(bf16[16,128,128]{2,1,0:T(8,128)(2,1)S(1)} %all-to-all-done.1.true_ref), channel_id=1, source_target_pairs={{128,0},{256,128},{384,256},{0,384},{129,1},{257,129},{385,257},{1... | collective-permute-start | bytes 1572872 | tf_op jit(solution)/shard_map/ppermute | solution.py:283
  40.0 0.7 copy-start.2
  40.7 10.5 %copy-start = (s32[8]{0:T(128)S(1)}, s32[8]{0:T(128)}, u32[]{:S(2)}) copy-start(s32[8]{0:T(128)} %offsets_ref.1) | copy-start | bytes 100

commit v2 on v0

--- a/solution.py
+++ b/solution.py
@@ -22,6 +22,8 @@
 BLOCK = GROUPS * COLS
 HALO = 14
 WINDOW = BLOCK + HALO * COLS
+AROUND = [8, 9, 10, 11, 12, 13, 0, 1, 2, 3, 4, 5, 6, 7, 14, 15]
+FIRST = (0 * 2 + 1) * K + 7
 MISSING = 1024.0
 LANES = 128
 
@@ -120,7 +122,7 @@
 
 
 def totals_at(k, t):
-    return pl.ds(pl.multiple_of((t * K + k) * 8, 8), 8)
+    return pl.ds(pl.multiple_of(((t * K + k - FIRST) & (GROUPS * K - 1)) * 8, 8), 8)
 
 
 def halves_of(value):
@@ -155,39 +157,37 @@
 
     def unpack(source, first):
         def tile(g, part, p, value, fore):
-            at = pl.ds(pl.multiple_of(g * WINDOW + first + p * COLS + part * 8, 8), 8)
+            at = pl.ds(g * WINDOW + first + p * COLS + part * 8, 8)
             keep = value < MISSING / 2
             shifted[at, :] = jnp.where(keep, value, 0.0)
             usable[at, :] = jnp.where(keep, 1.0, 0.0)
             if first == 0:
-                at = pl.ds(pl.multiple_of(g * BLOCK + p * COLS + part * 8, 8), 8)
+                at = pl.ds(g * BLOCK + p * COLS + part * 8, 8)
                 masked = jnp.where(keep, weight_ref[g : g + 1, :], 0.0)
                 scaled = fore * masked
                 weigh[at, :] = masked
                 cross[at, :] = scaled
                 spread[at, :] = scaled * fore
 
-        def run(p, carry):
+        for turn in range(source.shape[0]):
+            p = AROUND[turn]
             for g in range(STEPS):
                 rows = slice(g * COLS, (g + 1) * COLS)
-                value = source[p, rows, :].astype(jnp.float32)
-                fore = fore_ref[p, rows, :].astype(jnp.float32) if first == 0 else value
+                value = source[turn, rows, :].astype(jnp.float32)
+                fore = fore_ref[turn, rows, :].astype(jnp.float32) if first == 0 else value
                 for part in range(TILES):
                     tile(g, part, p, value[part * 8 : part * 8 + 8], fore[part * 8 : part * 8 + 8])
             rows = slice(STEPS * COLS, PACKED)
-            value = source[p, rows, :].astype(jnp.float32)
-            fore = fore_ref[p, rows, :].astype(jnp.float32) if first == 0 else value
+            value = source[turn, rows, :].astype(jnp.float32)
+            fore = fore_ref[turn, rows, :].astype(jnp.float32) if first == 0 else value
             for part in range(TILES):
-                turn = -PER * TAIL * part % LANES
-                moved = pltpu.roll(value, turn, 1) if part else value
+                shift = -PER * TAIL * part % LANES
+                moved = pltpu.roll(value, shift, 1) if part else value
                 moved = jnp.where(lane < PER * TAIL, moved, MISSING)
-                tile(STEPS, part, p, moved, pltpu.roll(fore, turn, 1) if part else fore)
-            return carry
-
-        return run
-
-    lax.fori_loop(0, GROUPS, unpack(true_ref, 0), 0, unroll=8)
-    lax.fori_loop(0, HALO, unpack(next_ref, BLOCK), 0, unroll=14)
+                tile(STEPS, part, p, moved, pltpu.roll(fore, shift, 1) if part else fore)
+
+    unpack(true_ref, 0)
+    unpack(next_ref, BLOCK)
     lag = [offsets_ref[k] for k in range(K)]
 
     def tile(t, carry):
@@ -236,9 +236,10 @@
     lane = lax.broadcasted_iota(jnp.int32, (8, LANES), 1)
     halves = [[jnp.zeros((8, LANES), jnp.float32)] * 2 for _ in range(3)]
     for q in range(GROUPS):
-        total = parts_ref[q * K].astype(jnp.float32)
-        for device in range(1, K):
-            total = total + parts_ref[q * K + device].astype(jnp.float32)
+        came = [(AROUND[q] * K + device - FIRST) % (GROUPS * K) for device in range(K)]
+        total = parts_ref[came[0]].astype(jnp.float32)
+        for at in came[1:]:
+            total = total + parts_ref[at].astype(jnp.float32)
         fore = pltpu.roll(total, LANES - 3 * PER, 1)
         true = pltpu.roll(total, LANES - 6 * PER, 1)
         value = total / jnp.sqrt((fore + REG) * (true + REG))
@@ -275,11 +276,11 @@
     flags = usable_point_flags.T
     around = ("y", "core")
     true = pack(observed_state, mean_state, flags)
-    true = lax.all_to_all(true, around, 0, 0, tiled=True)
+    true = lax.all_to_all(true, around, 0, 0, tiled=True, axis_index_groups=[AROUND])
     count = lax.axis_size("z")
     following = lax.ppermute(true[:HALO], "z", [((i + 1) % count, i) for i in range(count)])
     fore = pack(prediction, mean_state, flags)
-    fore = lax.all_to_all(fore, around, 0, 0, tiled=True)
+    fore = lax.all_to_all(fore, around, 0, 0, tiled=True, axis_index_groups=[AROUND])
     sums = window_call(
         sums_kernel,
         (eastward_offsets, weight, fore, true, following),
@@ -288,7 +289,8 @@
         20_000_000,
     )
     parts = sums.reshape(K * GROUPS, 8, LANES)
-    parts = lax.all_to_all(parts, around + ("lat",), 0, 0, tiled=True)
+    turned = [(i + FIRST) % (GROUPS * K) for i in range(GROUPS * K)]
+    parts = lax.all_to_all(parts, around + ("lat",), 0, 0, tiled=True, axis_index_groups=[turned])
     return finish(parts)
 
 

time: 91.7 us -> 83.6 us (0.912)
  blocking collectives: 34.4 us -> 26.1 us
  starting transfers between devices: 19.6 us -> 25.2 us
  waiting for transfers between devices: 23.7 us -> 18.1 us
    all_to_all x1, blocking collectives: 34.4 us -> 26.1 us  [local(): lax.all_to_all(parts, around + ('lat',), 0, 0, tiled=True, axis_index_gro...]
    all_to_all x2, starting transfers between devices: 13.7 us -> 20.9 us  [the longest x1 13.7 us: local(): lax.all_to_all(true, around, 0, 0, tiled=True, axis_index_groups=[AROUND])]
    all_to_all x2, waiting for transfers between devices: 23.7 us -> 17.3 us  [the longest x1 9.4 us: local(): lax.all_to_all(true, around, 0, 0, tiled=True, axis_index_groups=[AROUND])]
    ppermute x1, starting transfers between devices: 5.92 us -> 4.26 us  [local(): lax.ppermute(true[:HALO], 'z', [((i + 1) % count, i) for i in range(count)])]
  transfers between devices with their start and end apart: 3 -> 3, of which waited for: 2 -> 3; matrix products, arithmetic and copies ran while one was open for 0% -> 0% of each run, Pallas kernels for 4% -> 4%
where the time goes in v2:
time: 83.6 us; the launch traced here: 83.2 us
  blocking collectives  26.1 us (31%)
  starting transfers between devices  25.2 us (30%)
  waiting for transfers between devices  18.1 us (22%)
  Pallas kernels  13 us (16%)
    all_to_all x1, blocking collectives, local(): lax.all_to_all(parts, around + ('lat',), 0, 0, tiled=True, axis_index_gro...  26.1 us
    all_to_all x1, starting transfers between devices, local(): lax.all_to_all(true, around, 0, 0, tiled=True, axis_index_groups=[AROUND])  13.7 us
    all_to_all x1, waiting for transfers between devices, local(): lax.all_to_all(true, around, 0, 0, tiled=True, axis_index_groups=[AROUND])  9.4 us
    all_to_all x1, waiting for transfers between devices, local(): lax.all_to_all(fore, around, 0, 0, tiled=True, axis_index_groups=[AROUND])  7.92 us
    all_to_all x1, starting transfers between devices, local(): lax.all_to_all(fore, around, 0, 0, tiled=True, axis_index_groups=[AROUND])  7.22 us
    pallas_call x2, Pallas kernels, pack(): pl.pallas_call(pack_kernel, in_specs=[anywhere] * 3, out_specs=anywhere,...  7.08 us
    pallas_call x1, Pallas kernels, window_call(): pl.pallas_call(kernel, in_specs=[pl.BlockSpec(memory_space=pltpu.SMEM)] +...  5.11 us
    ppermute x1, starting transfers between devices, local(): lax.ppermute(true[:HALO], 'z', [((i + 1) % count, i) for i in range(count)])  4.26 us
  transfers between devices with their start and end apart: 3, of which 3 were waited for; matrix products, arithmetic and copies ran while one was open for 0% of the time, Pallas kernels for 4%

profile of v2, /device:TPU:1, one launch (start us, length us, event | category | flops | bytes accessed | tf_op | source)
XLA Modules:
  0.0 83.2 jit_solution(15067905552100074676)
XLA Ops:
  0.0 3.5 %pack.3 = bf16[16,128,128]{2,1,0:T(8,128)(2,1)} custom-call(bf16[48,24,222]{2,1,0:T(8,128)(2,1)} %field_ref.3, bf16[48,24,222]{2,1,0:T(8,128)(2,1)} %mean_ref.3, s32[24,48]{1,0:T(8,128)} %bitcast.3), custom_call_target="tpu_custom_call" | custom-call | flops 4000000 | bytes 2000000 | tf_op jit(solution)/shard_map/pack/pallas_call | solution.py:109
  3.5 13.7 %all-to-all-start.1 = ((bf16[16,128,128]{2,1,0:T(8,128)(2,1)}), bf16[16,128,128]{2,1,0:T(8,128)(2,1)S(1)}, u32[]{:S(2)}, u32[]{:S(2)}) async-start(bf16[16,128,128]{2,1,0:T(8,128)(2,1)} %pack.3), calls=%async_computation.1 | async-start | bytes 1048576 | tf_op jit(solution)/shard_map/all_to_all | solution.py:279
  17.2 3.6 %pack.2 = bf16[16,128,128]{2,1,0:T(8,128)(2,1)} custom-call(bf16[48,24,222]{2,1,0:T(8,128)(2,1)} %field_ref.2, bf16[48,24,222]{2,1,0:T(8,128)(2,1)} %mean_ref.3, s32[24,48]{1,0:T(8,128)} %bitcast.4), custom_call_target="tpu_custom_call" | custom-call | flops 4000000 | bytes 2000000 | tf_op jit(solution)/shard_map/pack/pallas_call | solution.py:109
  20.8 9.4 %all-to-all-done.1.true_ref = bf16[16,128,128]{2,1,0:T(8,128)(2,1)S(1)} async-done(((bf16[16,128,128]{2,1,0:T(8,128)(2,1)}), bf16[16,128,128]{2,1,0:T(8,128)(2,1)S(1)}, u32[]{:S(2)}, u32[]{:S(2)}) %all-to-all-start.1) | async-done | bytes 524320 | tf_op jit(solution)/shard_map/all_to_all | solution.py:279
  30.2 7.2 %all-to-all-start = ((bf16[16,128,128]{2,1,0:T(8,128)(2,1)}), bf16[16,128,128]{2,1,0:T(8,128)(2,1)S(1)}, u32[]{:S(2)}, u32[]{:S(2)}) async-start(bf16[16,128,128]{2,1,0:T(8,128)(2,1)} %pack.2), calls=%async_computation | async-start | bytes 1048576 | tf_op jit(solution)/shard_map/all_to_all | solution.py:283
  37.4 0.0 copy-start.1
  37.5 4.3 %collective-permute-start = (bf16[14,128,128]{2,1,0:T(8,128)(2,1)S(1)}, bf16[14,128,128]{2,1,0:T(8,128)(2,1)S(1)}, u32[]{:S(2)}, u32[]{:S(2)}) collective-permute-start(bf16[14,128,128]{2,1,0:T(8,128)(2,1)S(1)} %slice.4), channel_id=1, source_target_pairs={{128,0},{256,128},{384,256},{0,384},{129,1},{257,129},{385,257},{1... | collective-permute-start | bytes 1376264 | tf_op jit(solution)/shard_map/ppermute | solution.py:281
  41.7 0.0 copy-start.2
  41.7 0.0 copy-done.1
  41.7 0.7 copy-done.2
  42.4 0.0 copy-start
  42.5 7.9 %all-to-all-done.fore_ref = bf16[16,128,128]{2,1,0:T(8,128)(2,1)S(1)} async-done(((bf16[16,128,128]{2,1,0:T(8,128)(2,1)}), bf16[16,128,128]{2,1,0:T(8,128)(2,1)S(1)}, u32[]{:S(2)}, u32[]{:S(2)}) %all-to-all-start) | async-done | bytes 524320 | tf_op jit(solution)/shard_map/all_to_all | solution.py:283
  50.4 0.8 collective-permute-done.next_ref
  51.2 0.0 copy-done
  51.2 5.1 %lag_sums.1 = bf16[1024,128]{1,0:T(8,128)(2,1)S(1)} custom-call(s32[8]{0:T(128)S(1)} %copy-done, f32[6,128]{1,0:T(8,128)S(1)} %cosine_select_fusion.weight_ref, bf16[16,128,128]{2,1,0:T(8,128)(2,1)S(1)} %all-to-all-done.fore_ref, bf16[16,128,128]{2,1,0:T(8,128)(2,1)S(1)} %all-to-all-done.1.true_ref, bf16[14,128,128]{2,1,0:T(8,128)(2,1)S(1)} %collective-permute-done.next_ref), custom_call_target="tpu_custom_call" | custom-call | flops 20000000 | bytes 2000000 | tf_op jit(solution)/shard_map/lag_sums/pallas_call | solution.py:224
  56.3 26.1 %all_to_all.15.parts_ref = bf16[128,8,128]{2,1,0:T(8,128)(2,1)S(1)} all-to-all(bf16[128,8,128]{2,1,0:T(8,128)(2,1)S(1)} %bitcast.2), channel_id=1, replica_groups={{15,16,17,18,19,20,21,22,23,24,25,26,27,28,29,30,31,32,33,34,35,36,37,3..., dimensions={0} | all-to-all | bytes 524288 | tf_op jit(solution)/shard_map/all_to_all | solution.py:293
  82.4 0.8 finish.1
  (2 shorter events, 0.1 us)
Async XLA Ops:
  3.5 26.6 %all-to-all-start.1 = ((bf16[16,128,128]{2,1,0:T(8,128)(2,1)}), bf16[16,128,128]{2,1,0:T(8,128)(2,1)S(1)}, u32[]{:S(2)}, u32[]{:S(2)}) async-start(bf16[16,128,128]{2,1,0:T(8,128)(2,1)} %pack.3), calls=%async_computation.1 | async-start | bytes 1048576 | tf_op jit(solution)/shard_map/all_to_all | solution.py:279
  30.2 20.2 %all-to-all-start = ((bf16[16,128,128]{2,1,0:T(8,128)(2,1)}), bf16[16,128,128]{2,1,0:T(8,128)(2,1)S(1)}, u32[]{:S(2)}, u32[]{:S(2)}) async-start(bf16[16,128,128]{2,1,0:T(8,128)(2,1)} %pack.2), calls=%async_computation | async-start | bytes 1048576 | tf_op jit(solution)/shard_map/all_to_all | solution.py:283
  37.4 4.3 %copy-start.1 = (s32[6,128]{1,0:T(8,128)S(1)}, s32[6,128]{1,0:T(8,128)}, u32[]{:S(2)}) copy-start(s32[6,128]{1,0:T(8,128)} %constant.21.clone) | copy-start | bytes 9220
  37.5 13.7 %collective-permute-start = (bf16[14,128,128]{2,1,0:T(8,128)(2,1)S(1)}, bf16[14,128,128]{2,1,0:T(8,128)(2,1)S(1)}, u32[]{:S(2)}, u32[]{:S(2)}) collective-permute-start(bf16[14,128,128]{2,1,0:T(8,128)(2,1)S(1)} %slice.4), channel_id=1, source_target_pairs={{128,0},{256,128},{384,256},{0,384},{129,1},{257,129},{385,257},{1... | collective-permute-start | bytes 1376264 | tf_op jit(solution)/shard_map/ppermute | solution.py:281
  41.7 0.7 copy-start.2
  42.4 8.8 %copy-start = (s32[8]{0:T(128)S(1)}, s32[8]{0:T(128)}, u32[]{:S(2)}) copy-start(s32[8]{0:T(128)} %offsets_ref.1) | copy-start | bytes 100

commit v3 on v2

--- a/solution.py
+++ b/solution.py
@@ -22,8 +22,8 @@
 BLOCK = GROUPS * COLS
 HALO = 14
 WINDOW = BLOCK + HALO * COLS
-AROUND = [8, 9, 10, 11, 12, 13, 0, 1, 2, 3, 4, 5, 6, 7, 14, 15]
-FIRST = (0 * 2 + 1) * K + 7
+AROUND = [9, 8, 10, 11, 12, 13, 0, 1, 2, 3, 4, 5, 6, 7, 14, 15]
+FIRST = (4 * 2 + 1) * K + 5
 MISSING = 1024.0
 LANES = 128
 

time: 83.6 us -> 81 us (0.969)
  blocking collectives: 26.1 us -> 24.1 us
  starting transfers between devices: 25.2 us -> 24.3 us
    all_to_all x1, blocking collectives: 26.1 us -> 24.1 us  [local(): lax.all_to_all(parts, around + ('lat',), 0, 0, tiled=True, axis_index_gro...]
where the time goes in v3:
time: 81 us; the launch traced here: 80.5 us
  starting transfers between devices  24.3 us (30%)
  blocking collectives  24.1 us (30%)
  waiting for transfers between devices  18.3 us (23%)
  Pallas kernels  13 us (16%)
    all_to_all x1, blocking collectives, local(): lax.all_to_all(parts, around + ('lat',), 0, 0, tiled=True, axis_index_gro...  24.1 us
    all_to_all x1, starting transfers between devices, local(): lax.all_to_all(true, around, 0, 0, tiled=True, axis_index_groups=[AROUND])  13.4 us
    all_to_all x1, waiting for transfers between devices, local(): lax.all_to_all(true, around, 0, 0, tiled=True, axis_index_groups=[AROUND])  9.4 us
    all_to_all x1, waiting for transfers between devices, local(): lax.all_to_all(fore, around, 0, 0, tiled=True, axis_index_groups=[AROUND])  8.2 us
    pallas_call x2, Pallas kernels, pack(): pl.pallas_call(pack_kernel, in_specs=[anywhere] * 3, out_specs=anywhere,...  7.08 us
    all_to_all x1, starting transfers between devices, local(): lax.all_to_all(fore, around, 0, 0, tiled=True, axis_index_groups=[AROUND])  6.95 us
    pallas_call x1, Pallas kernels, window_call(): pl.pallas_call(kernel, in_specs=[pl.BlockSpec(memory_space=pltpu.SMEM)] +...  5.06 us
    ppermute x1, starting transfers between devices, local(): lax.ppermute(true[:HALO], 'z', [((i + 1) % count, i) for i in range(count)])  3.98 us
  transfers between devices with their start and end apart: 3, of which 3 were waited for; matrix products, arithmetic and copies ran while one was open for 0% of the time, Pallas kernels for 4%

profile of v3, /device:TPU:1, one launch (start us, length us, event | category | flops | bytes accessed | tf_op | source)
XLA Modules:
  0.0 80.5 jit_solution(7217339227663532841)
XLA Ops:
  0.0 3.5 %pack.3 = bf16[16,128,128]{2,1,0:T(8,128)(2,1)} custom-call(bf16[48,24,222]{2,1,0:T(8,128)(2,1)} %field_ref.3, bf16[48,24,222]{2,1,0:T(8,128)(2,1)} %mean_ref.3, s32[24,48]{1,0:T(8,128)} %bitcast.3), custom_call_target="tpu_custom_call" | custom-call | flops 4000000 | bytes 2000000 | tf_op jit(solution)/shard_map/pack/pallas_call | solution.py:109
  3.5 13.4 %all-to-all-start.1 = ((bf16[16,128,128]{2,1,0:T(8,128)(2,1)}), bf16[16,128,128]{2,1,0:T(8,128)(2,1)S(1)}, u32[]{:S(2)}, u32[]{:S(2)}) async-start(bf16[16,128,128]{2,1,0:T(8,128)(2,1)} %pack.3), calls=%async_computation.1 | async-start | bytes 1048576 | tf_op jit(solution)/shard_map/all_to_all | solution.py:279
  16.9 3.6 %pack.2 = bf16[16,128,128]{2,1,0:T(8,128)(2,1)} custom-call(bf16[48,24,222]{2,1,0:T(8,128)(2,1)} %field_ref.2, bf16[48,24,222]{2,1,0:T(8,128)(2,1)} %mean_ref.3, s32[24,48]{1,0:T(8,128)} %bitcast.4), custom_call_target="tpu_custom_call" | custom-call | flops 4000000 | bytes 2000000 | tf_op jit(solution)/shard_map/pack/pallas_call | solution.py:109
  20.5 9.4 %all-to-all-done.1.true_ref = bf16[16,128,128]{2,1,0:T(8,128)(2,1)S(1)} async-done(((bf16[16,128,128]{2,1,0:T(8,128)(2,1)}), bf16[16,128,128]{2,1,0:T(8,128)(2,1)S(1)}, u32[]{:S(2)}, u32[]{:S(2)}) %all-to-all-start.1) | async-done | bytes 524320 | tf_op jit(solution)/shard_map/all_to_all | solution.py:279
  29.9 6.9 %all-to-all-start = ((bf16[16,128,128]{2,1,0:T(8,128)(2,1)}), bf16[16,128,128]{2,1,0:T(8,128)(2,1)S(1)}, u32[]{:S(2)}, u32[]{:S(2)}) async-start(bf16[16,128,128]{2,1,0:T(8,128)(2,1)} %pack.2), calls=%async_computation | async-start | bytes 1048576 | tf_op jit(solution)/shard_map/all_to_all | solution.py:283
  36.9 0.0 copy-start.1
  36.9 4.0 %collective-permute-start = (bf16[14,128,128]{2,1,0:T(8,128)(2,1)S(1)}, bf16[14,128,128]{2,1,0:T(8,128)(2,1)S(1)}, u32[]{:S(2)}, u32[]{:S(2)}) collective-permute-start(bf16[14,128,128]{2,1,0:T(8,128)(2,1)S(1)} %slice.4), channel_id=1, source_target_pairs={{128,0},{256,128},{384,256},{0,384},{129,1},{257,129},{385,257},{1... | collective-permute-start | bytes 1376264 | tf_op jit(solution)/shard_map/ppermute | solution.py:281
  40.9 0.0 copy-start.2
  40.9 0.0 copy-done.1
  40.9 0.7 copy-done.2
  41.6 0.0 copy-start
  41.6 8.2 %all-to-all-done.fore_ref = bf16[16,128,128]{2,1,0:T(8,128)(2,1)S(1)} async-done(((bf16[16,128,128]{2,1,0:T(8,128)(2,1)}), bf16[16,128,128]{2,1,0:T(8,128)(2,1)S(1)}, u32[]{:S(2)}, u32[]{:S(2)}) %all-to-all-start) | async-done | bytes 524320 | tf_op jit(solution)/shard_map/all_to_all | solution.py:283
  49.8 0.7 collective-permute-done.next_ref
  50.5 0.0 copy-done
  50.5 5.1 %lag_sums.1 = bf16[1024,128]{1,0:T(8,128)(2,1)S(1)} custom-call(s32[8]{0:T(128)S(1)} %copy-done, f32[6,128]{1,0:T(8,128)S(1)} %cosine_select_fusion.weight_ref, bf16[16,128,128]{2,1,0:T(8,128)(2,1)S(1)} %all-to-all-done.fore_ref, bf16[16,128,128]{2,1,0:T(8,128)(2,1)S(1)} %all-to-all-done.1.true_ref, bf16[14,128,128]{2,1,0:T(8,128)(2,1)S(1)} %collective-permute-done.next_ref), custom_call_target="tpu_custom_call" | custom-call | flops 20000000 | bytes 2000000 | tf_op jit(solution)/shard_map/lag_sums/pallas_call | solution.py:224
  55.5 24.1 %all_to_all.15.parts_ref = bf16[128,8,128]{2,1,0:T(8,128)(2,1)S(1)} all-to-all(bf16[128,8,128]{2,1,0:T(8,128)(2,1)S(1)} %bitcast.2), channel_id=1, replica_groups={{77,78,79,80,81,82,83,84,85,86,87,88,89,90,91,92,93,94,95,96,97,98,99,1..., dimensions={0} | all-to-all | bytes 524288 | tf_op jit(solution)/shard_map/all_to_all | solution.py:293
  79.7 0.8 %finish.1 = f32[1,24,222]{2,1,0:T(8,128)} custom-call(bf16[128,8,128]{2,1,0:T(8,128)(2,1)S(1)} %all_to_all.15.parts_ref), custom_call_target="tpu_custom_call" | custom-call | flops 1000000 | bytes 2000000 | tf_op jit(solution)/shard_map/finish/pallas_call | solution.py:260
  (2 shorter events, 0.1 us)
Async XLA Ops:
  3.5 26.4 %all-to-all-start.1 = ((bf16[16,128,128]{2,1,0:T(8,128)(2,1)}), bf16[16,128,128]{2,1,0:T(8,128)(2,1)S(1)}, u32[]{:S(2)}, u32[]{:S(2)}) async-start(bf16[16,128,128]{2,1,0:T(8,128)(2,1)} %pack.3), calls=%async_computation.1 | async-start | bytes 1048576 | tf_op jit(solution)/shard_map/all_to_all | solution.py:279
  29.9 19.9 %all-to-all-start = ((bf16[16,128,128]{2,1,0:T(8,128)(2,1)}), bf16[16,128,128]{2,1,0:T(8,128)(2,1)S(1)}, u32[]{:S(2)}, u32[]{:S(2)}) async-start(bf16[16,128,128]{2,1,0:T(8,128)(2,1)} %pack.2), calls=%async_computation | async-start | bytes 1048576 | tf_op jit(solution)/shard_map/all_to_all | solution.py:283
  36.9 4.0 %copy-start.1 = (s32[6,128]{1,0:T(8,128)S(1)}, s32[6,128]{1,0:T(8,128)}, u32[]{:S(2)}) copy-start(s32[6,128]{1,0:T(8,128)} %constant.21.clone) | copy-start | bytes 9220
  36.9 13.6 %collective-permute-start = (bf16[14,128,128]{2,1,0:T(8,128)(2,1)S(1)}, bf16[14,128,128]{2,1,0:T(8,128)(2,1)S(1)}, u32[]{:S(2)}, u32[]{:S(2)}) collective-permute-start(bf16[14,128,128]{2,1,0:T(8,128)(2,1)S(1)} %slice.4), channel_id=1, source_target_pairs={{128,0},{256,128},{384,256},{0,384},{129,1},{257,129},{385,257},{1... | collective-permute-start | bytes 1376264 | tf_op jit(solution)/shard_map/ppermute | solution.py:281
  40.9 0.7 copy-start.2
  41.6 8.9 %copy-start = (s32[8]{0:T(128)S(1)}, s32[8]{0:T(128)}, u32[]{:S(2)}) copy-start(s32[8]{0:T(128)} %offsets_ref.1) | copy-start | bytes 100

commit v4 on v3

--- a/solution.py
+++ b/solution.py
@@ -1,3 +1,5 @@
+import functools
+
 import jax
 import jax.numpy as jnp
 import numpy as np
@@ -23,12 +25,13 @@
 HALO = 14
 WINDOW = BLOCK + HALO * COLS
 AROUND = [9, 8, 10, 11, 12, 13, 0, 1, 2, 3, 4, 5, 6, 7, 14, 15]
+NATURAL = list(range(16))
 FIRST = (4 * 2 + 1) * K + 5
 MISSING = 1024.0
 LANES = 128
 
 
-def pack_kernel(field_ref, mean_ref, flags_ref, out_ref, field, mean, flags, low, mid, high, packed, arrived, leaving):
+def pack_kernel(order, field_ref, mean_ref, flags_ref, out_ref, field, mean, flags, low, mid, high, packed, arrived, leaving):
     def rows_of(g):
         return pl.ds(g * SIDE, SIDE if g < STEPS else TAIL)
 
@@ -77,7 +80,8 @@
                 place(g % 2, slot, tile, left[rows], right[rows])
 
     def emit(g):
-        for q in range(GROUPS):
+        for to in range(GROUPS):
+            q = AROUND.index(order[to])
             source = low if q < 9 else mid if q == 9 else high
             slot = (lane - PER * q) & (LANES - 1)
             for part in range(TILES if g < STEPS else 1):
@@ -85,7 +89,7 @@
                 for at in range(1, SIDE):
                     acc = jnp.where(slot >= PER * at, source[g % 2, at, part], acc)
                 moved = pltpu.roll(acc, -PER * q % LANES, 1)
-                packed[q, pl.ds(g * COLS + part * 8, 8), :] = moved.astype(jnp.bfloat16)
+                packed[to, pl.ds(g * COLS + part * 8, 8), :] = moved.astype(jnp.bfloat16)
         leave(g).start()
 
     take(0)
@@ -104,10 +108,10 @@
     )
 
 
-def pack(field, mean, flags):
+def pack(field, mean, flags, order):
     anywhere = pl.BlockSpec(memory_space=pl.ANY)
     return pl.pallas_call(
-        pack_kernel,
+        functools.partial(pack_kernel, order),
         in_specs=[anywhere] * 3,
         out_specs=anywhere,
         out_shape=jax.ShapeDtypeStruct((GROUPS, PACKED, LANES), jnp.bfloat16),
@@ -174,12 +178,12 @@
             for g in range(STEPS):
                 rows = slice(g * COLS, (g + 1) * COLS)
                 value = source[turn, rows, :].astype(jnp.float32)
-                fore = fore_ref[turn, rows, :].astype(jnp.float32) if first == 0 else value
+                fore = fore_ref[p, rows, :].astype(jnp.float32) if first == 0 else value
                 for part in range(TILES):
                     tile(g, part, p, value[part * 8 : part * 8 + 8], fore[part * 8 : part * 8 + 8])
             rows = slice(STEPS * COLS, PACKED)
             value = source[turn, rows, :].astype(jnp.float32)
-            fore = fore_ref[turn, rows, :].astype(jnp.float32) if first == 0 else value
+            fore = fore_ref[p, rows, :].astype(jnp.float32) if first == 0 else value
             for part in range(TILES):
                 shift = -PER * TAIL * part % LANES
                 moved = pltpu.roll(value, shift, 1) if part else value
@@ -275,12 +279,12 @@
     weight = jnp.where(inside, weight, 0.0)
     flags = usable_point_flags.T
     around = ("y", "core")
-    true = pack(observed_state, mean_state, flags)
+    true = pack(observed_state, mean_state, flags, AROUND)
     true = lax.all_to_all(true, around, 0, 0, tiled=True, axis_index_groups=[AROUND])
     count = lax.axis_size("z")
     following = lax.ppermute(true[:HALO], "z", [((i + 1) % count, i) for i in range(count)])
-    fore = pack(prediction, mean_state, flags)
-    fore = lax.all_to_all(fore, around, 0, 0, tiled=True, axis_index_groups=[AROUND])
+    fore = pack(prediction, mean_state, flags, NATURAL)
+    fore = lax.all_to_all(fore, around, 0, 0, tiled=True, axis_index_groups=[NATURAL])
     sums = window_call(
         sums_kernel,
         (eastward_offsets, weight, fore, true, following),

time: 81 us -> 82.3 us (1.016)
  waiting for transfers between devices: 18.3 us -> 21.9 us
  blocking collectives: 24.1 us -> 22.1 us
    all_to_all x1, waiting for transfers between devices: 8.2 us -> 12.5 us  [local(): lax.all_to_all(fore, around, 0, 0, tiled=True, axis_index_groups=[NATURAL])]
    all_to_all x1, blocking collectives: 24.1 us -> 22.1 us  [local(): lax.all_to_all(parts, around + ('lat',), 0, 0, tiled=True, axis_index_gro...]
  transfers between devices with their start and end apart: 3 -> 3, of which waited for: 3 -> 2; matrix products, arithmetic and copies ran while one was open for 0% -> 0% of each run, Pallas kernels for 4% -> 4%
where the time goes in v4:
time: 82.3 us; the launch traced here: 82 us
  starting transfers between devices  24 us (29%)
  blocking collectives  22.1 us (27%)
  waiting for transfers between devices  21.9 us (27%)
  Pallas kernels  13.1 us (16%)
    all_to_all x1, blocking collectives, local(): lax.all_to_all(parts, around + ('lat',), 0, 0, tiled=True, axis_index_gro...  22.1 us
    all_to_all x1, starting transfers between devices, local(): lax.all_to_all(true, around, 0, 0, tiled=True, axis_index_groups=[AROUND])  13.4 us
    all_to_all x1, waiting for transfers between devices, local(): lax.all_to_all(fore, around, 0, 0, tiled=True, axis_index_groups=[NATURAL])  12.5 us
    all_to_all x1, waiting for transfers between devices, local(): lax.all_to_all(true, around, 0, 0, tiled=True, axis_index_groups=[AROUND])  9.4 us
    pallas_call x2, Pallas kernels, pack(): pl.pallas_call(functools.partial(pack_kernel, order), in_specs=[anywhere]...  7.09 us
    all_to_all x1, starting transfers between devices, local(): lax.all_to_all(fore, around, 0, 0, tiled=True, axis_index_groups=[NATURAL])  6.67 us
    pallas_call x1, Pallas kernels, window_call(): pl.pallas_call(kernel, in_specs=[pl.BlockSpec(memory_space=pltpu.SMEM)] +...  5.23 us
    ppermute x1, starting transfers between devices, local(): lax.ppermute(true[:HALO], 'z', [((i + 1) % count, i) for i in range(count)])  3.95 us
  transfers between devices with their start and end apart: 3, of which 2 were waited for; matrix products, arithmetic and copies ran while one was open for 0% of the time, Pallas kernels for 4%

profile of v4, /device:TPU:1, one launch (start us, length us, event | category | flops | bytes accessed | tf_op | source)
XLA Modules:
  0.0 82.0 jit_solution(2981142603375398603)
XLA Ops:
  0.0 3.5 %pack.3 = bf16[16,128,128]{2,1,0:T(8,128)(2,1)} custom-call(bf16[48,24,222]{2,1,0:T(8,128)(2,1)} %field_ref.3, bf16[48,24,222]{2,1,0:T(8,128)(2,1)} %mean_ref.3, s32[24,48]{1,0:T(8,128)} %bitcast.3), custom_call_target="tpu_custom_call" | custom-call | flops 4000000 | bytes 2000000 | tf_op jit(solution)/shard_map/pack/pallas_call | solution.py:113
  3.5 13.4 %all-to-all-start.1 = ((bf16[16,128,128]{2,1,0:T(8,128)(2,1)}), bf16[16,128,128]{2,1,0:T(8,128)(2,1)S(1)}, u32[]{:S(2)}, u32[]{:S(2)}) async-start(bf16[16,128,128]{2,1,0:T(8,128)(2,1)} %pack.3), calls=%async_computation.1 | async-start | bytes 1048576 | tf_op jit(solution)/shard_map/all_to_all | solution.py:283
  16.9 3.6 %pack.2 = bf16[16,128,128]{2,1,0:T(8,128)(2,1)} custom-call(bf16[48,24,222]{2,1,0:T(8,128)(2,1)} %field_ref.2, bf16[48,24,222]{2,1,0:T(8,128)(2,1)} %mean_ref.3, s32[24,48]{1,0:T(8,128)} %bitcast.4), custom_call_target="tpu_custom_call" | custom-call | flops 4000000 | bytes 2000000 | tf_op jit(solution)/shard_map/pack/pallas_call | solution.py:113
  20.5 9.4 %all-to-all-done.1.true_ref = bf16[16,128,128]{2,1,0:T(8,128)(2,1)S(1)} async-done(((bf16[16,128,128]{2,1,0:T(8,128)(2,1)}), bf16[16,128,128]{2,1,0:T(8,128)(2,1)S(1)}, u32[]{:S(2)}, u32[]{:S(2)}) %all-to-all-start.1) | async-done | bytes 524320 | tf_op jit(solution)/shard_map/all_to_all | solution.py:283
  29.9 6.7 %all-to-all-start = ((bf16[16,128,128]{2,1,0:T(8,128)(2,1)}), bf16[16,128,128]{2,1,0:T(8,128)(2,1)S(1)}, u32[]{:S(2)}, u32[]{:S(2)}) async-start(bf16[16,128,128]{2,1,0:T(8,128)(2,1)} %pack.2), calls=%async_computation | async-start | bytes 1048576 | tf_op jit(solution)/shard_map/all_to_all | solution.py:287
  36.6 0.0 copy-start.1
  36.6 3.9 %collective-permute-start = (bf16[14,128,128]{2,1,0:T(8,128)(2,1)S(1)}, bf16[14,128,128]{2,1,0:T(8,128)(2,1)S(1)}, u32[]{:S(2)}, u32[]{:S(2)}) collective-permute-start(bf16[14,128,128]{2,1,0:T(8,128)(2,1)S(1)} %slice.4), channel_id=1, source_target_pairs={{128,0},{256,128},{384,256},{0,384},{129,1},{257,129},{385,257},{1... | collective-permute-start | bytes 1376264 | tf_op jit(solution)/shard_map/ppermute | solution.py:285
  40.6 0.0 copy-start.2
  40.6 0.0 copy-done.1
  40.6 0.7 copy-done.2
  41.3 0.0 copy-start
  41.3 12.5 %all-to-all-done.fore_ref = bf16[16,128,128]{2,1,0:T(8,128)(2,1)S(1)} async-done(((bf16[16,128,128]{2,1,0:T(8,128)(2,1)}), bf16[16,128,128]{2,1,0:T(8,128)(2,1)S(1)}, u32[]{:S(2)}, u32[]{:S(2)}) %all-to-all-start) | async-done | bytes 524320 | tf_op jit(solution)/shard_map/all_to_all | solution.py:287
  53.8 0.0 collective-permute-done.next_ref
  53.8 0.0 copy-done
  53.8 5.2 %lag_sums.1 = bf16[1024,128]{1,0:T(8,128)(2,1)S(1)} custom-call(s32[8]{0:T(128)S(1)} %copy-done, f32[6,128]{1,0:T(8,128)S(1)} %cosine_select_fusion.weight_ref, bf16[16,128,128]{2,1,0:T(8,128)(2,1)S(1)} %all-to-all-done.fore_ref, bf16[16,128,128]{2,1,0:T(8,128)(2,1)S(1)} %all-to-all-done.1.true_ref, bf16[14,128,128]{2,1,0:T(8,128)(2,1)S(1)} %collective-permute-done.next_ref), custom_call_target="tpu_custom_call" | custom-call | flops 20000000 | bytes 2000000 | tf_op jit(solution)/shard_map/lag_sums/pallas_call | solution.py:228
  59.0 22.1 %all_to_all.15.parts_ref = bf16[128,8,128]{2,1,0:T(8,128)(2,1)S(1)} all-to-all(bf16[128,8,128]{2,1,0:T(8,128)(2,1)S(1)} %bitcast.2), channel_id=1, replica_groups={{77,78,79,80,81,82,83,84,85,86,87,88,89,90,91,92,93,94,95,96,97,98,99,1..., dimensions={0} | all-to-all | bytes 524288 | tf_op jit(solution)/shard_map/all_to_all | solution.py:297
  81.2 0.8 finish.1
  (2 shorter events, 0.1 us)
Async XLA Ops:
  3.5 26.4 %all-to-all-start.1 = ((bf16[16,128,128]{2,1,0:T(8,128)(2,1)}), bf16[16,128,128]{2,1,0:T(8,128)(2,1)S(1)}, u32[]{:S(2)}, u32[]{:S(2)}) async-start(bf16[16,128,128]{2,1,0:T(8,128)(2,1)} %pack.3), calls=%async_computation.1 | async-start | bytes 1048576 | tf_op jit(solution)/shard_map/all_to_all | solution.py:283
  29.9 23.9 %all-to-all-start = ((bf16[16,128,128]{2,1,0:T(8,128)(2,1)}), bf16[16,128,128]{2,1,0:T(8,128)(2,1)S(1)}, u32[]{:S(2)}, u32[]{:S(2)}) async-start(bf16[16,128,128]{2,1,0:T(8,128)(2,1)} %pack.2), calls=%async_computation | async-start | bytes 1048576 | tf_op jit(solution)/shard_map/all_to_all | solution.py:287
  36.6 4.0 %copy-start.1 = (s32[6,128]{1,0:T(8,128)S(1)}, s32[6,128]{1,0:T(8,128)}, u32[]{:S(2)}) copy-start(s32[6,128]{1,0:T(8,128)} %constant.21.clone) | copy-start | bytes 9220
  36.6 17.2 %collective-permute-start = (bf16[14,128,128]{2,1,0:T(8,128)(2,1)S(1)}, bf16[14,128,128]{2,1,0:T(8,128)(2,1)S(1)}, u32[]{:S(2)}, u32[]{:S(2)}) collective-permute-start(bf16[14,128,128]{2,1,0:T(8,128)(2,1)S(1)} %slice.4), channel_id=1, source_target_pairs={{128,0},{256,128},{384,256},{0,384},{129,1},{257,129},{385,257},{1... | collective-permute-start | bytes 1376264 | tf_op jit(solution)/shard_map/ppermute | solution.py:285
  40.6 0.7 copy-start.2
  41.3 12.5 %copy-start = (s32[8]{0:T(128)S(1)}, s32[8]{0:T(128)}, u32[]{:S(2)}) copy-start(s32[8]{0:T(128)} %offsets_ref.1) | copy-start | bytes 100

commit v5 on v3

--- a/solution.py
+++ b/solution.py
@@ -23,7 +23,7 @@
 HALO = 14
 WINDOW = BLOCK + HALO * COLS
 AROUND = [9, 8, 10, 11, 12, 13, 0, 1, 2, 3, 4, 5, 6, 7, 14, 15]
-FIRST = (4 * 2 + 1) * K + 5
+FIRST = 5
 MISSING = 1024.0
 LANES = 128
 
@@ -122,7 +122,7 @@
 
 
 def totals_at(k, t):
-    return pl.ds(pl.multiple_of(((t * K + k - FIRST) & (GROUPS * K - 1)) * 8, 8), 8)
+    return pl.ds(pl.multiple_of(((k - FIRST) % K * GROUPS + t) * 8, 8), 8)
 
 
 def halves_of(value):
@@ -232,17 +232,21 @@
     )(*inputs)
 
 
-def finish_kernel(parts_ref, out_ref):
+def correlate_kernel(parts_ref, out_ref):
+    for block in range(GROUPS):
+        total = parts_ref[0, block].astype(jnp.float32)
+        for device in range(1, K):
+            total = total + parts_ref[device, block].astype(jnp.float32)
+        fore = pltpu.roll(total, LANES - 3 * PER, 1)
+        true = pltpu.roll(total, LANES - 6 * PER, 1)
+        out_ref[AROUND.index(block)] = total / jnp.sqrt((fore + REG) * (true + REG))
+
+
+def finish_kernel(values_ref, out_ref):
     lane = lax.broadcasted_iota(jnp.int32, (8, LANES), 1)
     halves = [[jnp.zeros((8, LANES), jnp.float32)] * 2 for _ in range(3)]
     for q in range(GROUPS):
-        came = [(AROUND[q] * K + device - FIRST) % (GROUPS * K) for device in range(K)]
-        total = parts_ref[came[0]].astype(jnp.float32)
-        for at in came[1:]:
-            total = total + parts_ref[at].astype(jnp.float32)
-        fore = pltpu.roll(total, LANES - 3 * PER, 1)
-        true = pltpu.roll(total, LANES - 6 * PER, 1)
-        value = total / jnp.sqrt((fore + REG) * (true + REG))
+        value = values_ref[q]
         low, high = PER * q, PER * q + PER
         for part in range(3):
             moved = pltpu.roll(value, (PER * q - PER * part) % LANES, 1)
@@ -255,16 +259,16 @@
         out_ref[0, part * 8 : part * 8 + 8, LANES:] = halves[part][1][:, : CHANNELS - LANES]
 
 
-def finish(parts):
+def small_call(kernel, value, shape, name):
     vmem = pl.BlockSpec(memory_space=pltpu.VMEM)
     return pl.pallas_call(
-        finish_kernel,
+        kernel,
         in_specs=[vmem],
         out_specs=vmem,
-        out_shape=jax.ShapeDtypeStruct((1, COLS, CHANNELS), jnp.float32),
-        name="finish",
+        out_shape=jax.ShapeDtypeStruct(shape, jnp.float32),
+        name=name,
         **on_chip(4, 1_000_000),
-    )(parts)
+    )(value)
 
 
 def local(prediction, observed_state, mean_state, usable_point_flags, eastward_offsets):
@@ -288,10 +292,12 @@
         "lag_sums",
         20_000_000,
     )
-    parts = sums.reshape(K * GROUPS, 8, LANES)
-    turned = [(i + FIRST) % (GROUPS * K) for i in range(GROUPS * K)]
-    parts = lax.all_to_all(parts, around + ("lat",), 0, 0, tiled=True, axis_index_groups=[turned])
-    return finish(parts)
+    parts = sums.reshape(K, GROUPS, 8, LANES)
+    turned = [(i + FIRST) % K for i in range(K)]
+    parts = lax.all_to_all(parts, "lat", 0, 0, tiled=True, axis_index_groups=[turned])
+    values = small_call(correlate_kernel, parts, (GROUPS, 8, LANES), "correlate")
+    values = lax.all_to_all(values, around, 0, 0, tiled=True, axis_index_groups=[AROUND])
+    return small_call(finish_kernel, values, (1, COLS, CHANNELS), "finish")
 
 
 def solution(mesh):

time: 81 us -> 82.4 us (1.017)
  blocking collectives: 24.1 us -> 25.6 us
    all_to_all x1 -> x2, blocking collectives: 24.1 us -> 25.6 us  [the longest x1 13.9 us: local(): lax.all_to_all(parts, 'lat', 0, 0, tiled=True, axis_index_groups=[turned])]
where the time goes in v5:
time: 82.4 us; the launch traced here: 81.9 us
  blocking collectives  25.6 us (31%)
  starting transfers between devices  24.3 us (29%)
  waiting for transfers between devices  18.3 us (22%)
  Pallas kernels  13 us (16%)
    all_to_all x1, blocking collectives, local(): lax.all_to_all(parts, 'lat', 0, 0, tiled=True, axis_index_groups=[turned])  13.9 us
    all_to_all x1, starting transfers between devices, local(): lax.all_to_all(true, around, 0, 0, tiled=True, axis_index_groups=[AROUND])  13.4 us
    all_to_all x1, blocking collectives, local(): lax.all_to_all(values, around, 0, 0, tiled=True, axis_index_groups=[AROUND])  11.7 us
    all_to_all x1, waiting for transfers between devices, local(): lax.all_to_all(true, around, 0, 0, tiled=True, axis_index_groups=[AROUND])  9.4 us
    all_to_all x1, waiting for transfers between devices, local(): lax.all_to_all(fore, around, 0, 0, tiled=True, axis_index_groups=[AROUND])  8.2 us
    pallas_call x2, Pallas kernels, pack(): pl.pallas_call(pack_kernel, in_specs=[anywhere] * 3, out_specs=anywhere,...  7.08 us
    all_to_all x1, starting transfers between devices, local(): lax.all_to_all(fore, around, 0, 0, tiled=True, axis_index_groups=[AROUND])  6.95 us
    pallas_call x1, Pallas kernels, window_call(): pl.pallas_call(kernel, in_specs=[pl.BlockSpec(memory_space=pltpu.SMEM)] +...  5.02 us
  transfers between devices with their start and end apart: 3, of which 3 were waited for; matrix products, arithmetic and copies ran while one was open for 0% of the time, Pallas kernels for 4%

profile of v5, /device:TPU:1, one launch (start us, length us, event | category | flops | bytes accessed | tf_op | source)
XLA Modules:
  0.0 81.9 jit_solution(7271565127759095165)
XLA Ops:
  0.0 3.5 %pack.3 = bf16[16,128,128]{2,1,0:T(8,128)(2,1)} custom-call(bf16[48,24,222]{2,1,0:T(8,128)(2,1)} %field_ref.3, bf16[48,24,222]{2,1,0:T(8,128)(2,1)} %mean_ref.3, s32[24,48]{1,0:T(8,128)} %bitcast.3), custom_call_target="tpu_custom_call" | custom-call | flops 4000000 | bytes 2000000 | tf_op jit(solution)/shard_map/pack/pallas_call | solution.py:109
  3.5 13.4 %all-to-all-start.1 = ((bf16[16,128,128]{2,1,0:T(8,128)(2,1)}), bf16[16,128,128]{2,1,0:T(8,128)(2,1)S(1)}, u32[]{:S(2)}, u32[]{:S(2)}) async-start(bf16[16,128,128]{2,1,0:T(8,128)(2,1)} %pack.3), calls=%async_computation.1 | async-start | bytes 1048576 | tf_op jit(solution)/shard_map/all_to_all | solution.py:283
  16.9 3.6 %pack.2 = bf16[16,128,128]{2,1,0:T(8,128)(2,1)} custom-call(bf16[48,24,222]{2,1,0:T(8,128)(2,1)} %field_ref.2, bf16[48,24,222]{2,1,0:T(8,128)(2,1)} %mean_ref.3, s32[24,48]{1,0:T(8,128)} %bitcast.4), custom_call_target="tpu_custom_call" | custom-call | flops 4000000 | bytes 2000000 | tf_op jit(solution)/shard_map/pack/pallas_call | solution.py:109
  20.5 9.4 %all-to-all-done.1.true_ref = bf16[16,128,128]{2,1,0:T(8,128)(2,1)S(1)} async-done(((bf16[16,128,128]{2,1,0:T(8,128)(2,1)}), bf16[16,128,128]{2,1,0:T(8,128)(2,1)S(1)}, u32[]{:S(2)}, u32[]{:S(2)}) %all-to-all-start.1) | async-done | bytes 524320 | tf_op jit(solution)/shard_map/all_to_all | solution.py:283
  29.9 6.9 %all-to-all-start = ((bf16[16,128,128]{2,1,0:T(8,128)(2,1)}), bf16[16,128,128]{2,1,0:T(8,128)(2,1)S(1)}, u32[]{:S(2)}, u32[]{:S(2)}) async-start(bf16[16,128,128]{2,1,0:T(8,128)(2,1)} %pack.2), calls=%async_computation | async-start | bytes 1048576 | tf_op jit(solution)/shard_map/all_to_all | solution.py:287
  36.9 0.0 copy-start.1
  36.9 4.0 %collective-permute-start = (bf16[14,128,128]{2,1,0:T(8,128)(2,1)S(1)}, bf16[14,128,128]{2,1,0:T(8,128)(2,1)S(1)}, u32[]{:S(2)}, u32[]{:S(2)}) collective-permute-start(bf16[14,128,128]{2,1,0:T(8,128)(2,1)S(1)} %slice.4), channel_id=1, source_target_pairs={{128,0},{256,128},{384,256},{0,384},{129,1},{257,129},{385,257},{1... | collective-permute-start | bytes 1376264 | tf_op jit(solution)/shard_map/ppermute | solution.py:285
  40.9 0.0 copy-start.2
  40.9 0.0 copy-done.1
  40.9 0.7 copy-done.2
  41.6 0.0 copy-start
  41.6 8.2 %all-to-all-done.fore_ref = bf16[16,128,128]{2,1,0:T(8,128)(2,1)S(1)} async-done(((bf16[16,128,128]{2,1,0:T(8,128)(2,1)}), bf16[16,128,128]{2,1,0:T(8,128)(2,1)S(1)}, u32[]{:S(2)}, u32[]{:S(2)}) %all-to-all-start) | async-done | bytes 524320 | tf_op jit(solution)/shard_map/all_to_all | solution.py:287
  49.8 0.7 collective-permute-done.next_ref
  50.5 0.0 copy-done
  50.5 5.0 %lag_sums.1 = bf16[1024,128]{1,0:T(8,128)(2,1)S(1)} custom-call(s32[8]{0:T(128)S(1)} %copy-done, f32[6,128]{1,0:T(8,128)S(1)} %cosine_select_fusion.weight_ref, bf16[16,128,128]{2,1,0:T(8,128)(2,1)S(1)} %all-to-all-done.fore_ref, bf16[16,128,128]{2,1,0:T(8,128)(2,1)S(1)} %all-to-all-done.1.true_ref, bf16[14,128,128]{2,1,0:T(8,128)(2,1)S(1)} %collective-permute-done.next_ref), custom_call_target="tpu_custom_call" | custom-call | flops 20000000 | bytes 2000000 | tf_op jit(solution)/shard_map/lag_sums/pallas_call | solution.py:224
  55.5 13.9 %all_to_all.20.parts_ref = bf16[8,16,8,128]{3,2,1,0:T(8,128)(2,1)S(1)} all-to-all(bf16[8,16,8,128]{3,2,1,0:T(8,128)(2,1)S(1)} %bitcast.2), channel_id=1, replica_groups={{5,6,7,0,1,2,3,4},{13,14,15,8,9,10,11,12},{21,22,23,16,17,18,19,20},{29..., dimensions={0} | all-to-all | bytes 524288 | tf_op jit(solution)/shard_map/all_to_all | solution.py:297
  69.4 0.1 correlate.1
  69.5 11.7 %all_to_all.21.values_ref = f32[16,8,128]{2,1,0:T(8,128)S(1)} all-to-all(f32[16,8,128]{2,1,0:T(8,128)S(1)} %correlate.1), channel_id=1, replica_groups={{72,64,80,88,96,104,0,8,16,24,32,40,48,56,112,120},{73,65,81,89,97,105,..., dimensions={0} | all-to-all | bytes 131072 | tf_op jit(solution)/shard_map/all_to_all | solution.py:299
  81.2 0.7 finish.1
  (2 shorter events, 0.1 us)
Async XLA Ops:
  3.5 26.4 %all-to-all-start.1 = ((bf16[16,128,128]{2,1,0:T(8,128)(2,1)}), bf16[16,128,128]{2,1,0:T(8,128)(2,1)S(1)}, u32[]{:S(2)}, u32[]{:S(2)}) async-start(bf16[16,128,128]{2,1,0:T(8,128)(2,1)} %pack.3), calls=%async_computation.1 | async-start | bytes 1048576 | tf_op jit(solution)/shard_map/all_to_all | solution.py:283
  29.9 19.9 %all-to-all-start = ((bf16[16,128,128]{2,1,0:T(8,128)(2,1)}), bf16[16,128,128]{2,1,0:T(8,128)(2,1)S(1)}, u32[]{:S(2)}, u32[]{:S(2)}) async-start(bf16[16,128,128]{2,1,0:T(8,128)(2,1)} %pack.2), calls=%async_computation | async-start | bytes 1048576 | tf_op jit(solution)/shard_map/all_to_all | solution.py:287
  36.9 4.0 %copy-start.1 = (s32[6,128]{1,0:T(8,128)S(1)}, s32[6,128]{1,0:T(8,128)}, u32[]{:S(2)}) copy-start(s32[6,128]{1,0:T(8,128)} %constant.21.clone) | copy-start | bytes 9220
  36.9 13.6 %collective-permute-start = (bf16[14,128,128]{2,1,0:T(8,128)(2,1)S(1)}, bf16[14,128,128]{2,1,0:T(8,128)(2,1)S(1)}, u32[]{:S(2)}, u32[]{:S(2)}) collective-permute-start(bf16[14,128,128]{2,1,0:T(8,128)(2,1)S(1)} %slice.4), channel_id=1, source_target_pairs={{128,0},{256,128},{384,256},{0,384},{129,1},{257,129},{385,257},{1... | collective-permute-start | bytes 1376264 | tf_op jit(solution)/shard_map/ppermute | solution.py:285
  40.9 0.7 copy-start.2
  41.6 8.9 %copy-start = (s32[8]{0:T(128)S(1)}, s32[8]{0:T(128)}, u32[]{:S(2)}) copy-start(s32[8]{0:T(128)} %offsets_ref.1) | copy-start | bytes 100
